TPU v7x, 32 devices: a whole 2x2x4 slice. The times are simulated.
32 devices in a mesh: curve: 4 (over y, core), group: 8 (over z, x).
Axes of the slice: x: 2, y: 2, z: 4, core: 2. Of those that a mesh axis runs over, the one named last changes fastest.
Arguments:
- right_side: float32 [125, 16384], P(None, ('curve', 'group')), may hold values from -6 to 6, as said below
- conductivity: float32 [16384], P(('curve', 'group')), may hold values from 0.3 to 3
- destination: int32 [16384], P(('curve', 'group')), may hold values from 0 to 16383, as said below
- neighbour: int32 [6, 16384], P(None, ('curve', 'group')), may hold values from -1 to 1023, as said below
- orientation: int32 [6, 16384], P(None, ('curve', 'group')), may hold values from 0 to 3, as said below
- send_list: int32 [2, 8192], P(None, ('curve', 'group')), may hold values from 0 to 511, as said below
Outputs:
- solution: float32 [125, 16384], P(None, ('curve', 'group'))
- residual: float32 [125, 16384], P(None, ('curve', 'group'))
Inputs may be any that keep to these rules, and one draw needn't show every extreme that they name: `right_side`: custom normal-like values. `destination`: A permutation of all cells. Devices are ordered along the curve with curve slowest; every cell's new device is its old device or the one just before or after it. From each device at most 64 cells go to the next device and exactly as many come back from it; 64 is reached at some pair of neighbouring devices in every draw. `neighbour`: values below 512 are local cells of the same device. Only face 0 may name a slot from 512 to 512 + 256 - 1 (filled by the previous device from its send_list row 1), only face 1 a slot from 768 up (filled by the next device from its send_list row 0). Faces are paired: the cell across face f sees this cell across face f xor 1. -1 only at the domain boundary; the first device has no partner across its face 0 slots and the last none across face 1 slots. `orientation`: both sides of a shared face carry the same code; ignored where neighbour is -1. `send_list`: per device 256 distinct local cells in each row.
All inputs are finite; a program needn't handle non-finite values.
Results may differ from a plain program's by a relative error of at most 0.00015.
Values sent between devices are 32-bit elements; how exact they have to be, the bound alone decides.
A program may use at most 64 MiB of HBM per device.

v0:
```python
import functools

import jax
import jax.numpy as jnp
import numpy as np
from jax import lax
from jax.experimental import pallas as pl
from jax.experimental.pallas import tpu as pltpu
from jax.sharding import PartitionSpec as P

NODES = 5
BLOCK = 125
MOVE = 64
PENALTY = 80.0
MESH = pl.DeviceIdType.MESH
BF = jnp.bfloat16
F32 = jnp.float32

ROWS = 128
KAPPA = 125
TAG = 126
PART = 32
FACE = 2 * PART
FACE_KAPPA = 25

GAUSS_POINTS = (-0.906179845938664, -0.5384693101056831, 0.0, 0.5384693101056831, 0.906179845938664)
GAUSS_WEIGHTS = (
    0.2369268850561891,
    0.4786286704993665,
    0.5688888888888889,
    0.4786286704993665,
    0.2369268850561891,
)


def lagrange_value(points, position, location):
    out = 1.0
    for other in range(len(points)):
        if other != position:
            out = out * (location - points[other]) / (points[position] - points[other])
    return out


def lagrange_slope(points, position, location):
    total = 0.0
    for skipped in range(len(points)):
        if skipped == position:
            continue
        addend = 1.0 / (points[position] - points[skipped])
        for other in range(len(points)):
            if other != position and other != skipped:
                addend = addend * (location - points[other]) / (points[position] - points[other])
        total = total + addend
    return total


def along_axis(matrix, axis):
    five = np.eye(NODES)
    plane = np.eye(NODES * NODES)
    if axis == 0:
        return np.kron(matrix, plane)
    if axis == 1:
        return np.kron(five, np.kron(matrix, five))
    return np.kron(plane, matrix)


def split_table(table):
    high = table.astype(BF)
    low = (table - high.astype(np.float64)).astype(BF)
    return high, low


def tables():
    points = [0.5 * (value + 1.0) for value in GAUSS_POINTS]
    weights = np.array([0.5 * value for value in GAUSS_WEIGHTS])
    slopes = np.array([[lagrange_slope(points, p, points[q]) for p in range(NODES)] for q in range(NODES)])
    ends = [np.array([lagrange_value(points, p, at) for p in range(NODES)]) for at in (0.0, 1.0)]
    normals = [
        np.array([sign * lagrange_slope(points, p, at) for p in range(NODES)])
        for sign, at in ((-1.0, 0.0), (1.0, 1.0))
    ]
    cell_weight = np.kron(weights, np.kron(weights, weights))
    stiffness = np.zeros((BLOCK, BLOCK))
    for axis in range(3):
        grad = along_axis(slopes, axis)
        stiffness += grad.T @ (cell_weight[:, None] * grad)
    half = np.sqrt(0.5)
    parity_rows = np.zeros((NODES, NODES))
    for row, (a, b, sign) in enumerate(((0, 4, 1), (1, 3, 1), (2, 2, 1), (0, 4, -1), (1, 3, -1))):
        if a == b:
            parity_rows[row, a] = 1.0
        else:
            parity_rows[row, a] = half
            parity_rows[row, b] = sign * half
    parity = np.array([0, 0, 0, 1, 1])
    row_weight = weights[[0, 1, 2, 0, 1]]
    both = np.kron(parity_rows, parity_rows)
    count = NODES * NODES
    trace = np.zeros((6 * FACE, ROWS))
    for face in range(6):
        start = face * FACE
        trace[start : start + count, :BLOCK] = both @ along_axis(ends[face % 2][None, :], face // 2)
        trace[start + PART : start + PART + count, :BLOCK] = both @ along_axis(
            normals[face % 2][None, :], face // 2
        )
    lift = trace.T.copy()
    for face in range(6):
        trace[face * FACE + FACE_KAPPA, KAPPA] = 1.0
    first = np.zeros((6 * FACE + ROWS, ROWS))
    first[: 6 * FACE] = trace
    first[6 * FACE : 6 * FACE + BLOCK, :BLOCK] = stiffness
    high, low = split_table(first)
    forward = np.concatenate([high, high, low], 1)
    high, low = split_table(lift)
    backward = np.concatenate([high, low], 0)
    columns = np.zeros((ROWS, ROWS), np.float32)
    columns[:BLOCK, 0] = cell_weight
    columns[:count, 1] = np.kron(row_weight, row_weight)
    columns[:count, 2] = 2.0 * np.kron(parity, np.ones(NODES))
    columns[:count, 3] = 2.0 * np.kron(np.ones(NODES), parity)
    return forward, backward, columns


def split_two(value):
    high = value.astype(BF)
    low = (value - high.astype(F32)).astype(BF)
    return high, low


def split_three(value):
    high = value.astype(BF)
    rest = value - high.astype(F32)
    mid = rest.astype(BF)
    return high, mid, (rest - mid.astype(F32)).astype(BF)


def one_hot(left, right):
    return jnp.where(left == right, 1.0, 0.0).astype(BF)


def dot(left, right):
    return jnp.dot(left, right, preferred_element_type=F32)


def dot_last(left, right):
    return lax.dot_general(left, right, (((1,), (1,)), ((), ())), preferred_element_type=F32)


def iota(shape, dim):
    return lax.broadcasted_iota(jnp.int32, shape, dim)


def kernel(
    shape,
    rhs_ref,
    cond_ref,
    dest_ref,
    neigh_ref,
    orient_ref,
    list_ref,
    forward_ref,
    backward_ref,
    column_ref,
    x_ref,
    r_ref,
    payload,
    local_hot,
    ghost_hot,
    send_hot,
    packed,
    moved,
    halo_out,
    halo_in,
    sums,
    move_send,
    move_recv,
    halo_send,
    halo_recv,
    sum_send,
    sum_recv,
):
    curve, group = shape
    ranks = curve * group
    cells = rhs_ref.shape[1]
    ghost = list_ref.shape[1]
    me = lax.axis_index("curve") * group + lax.axis_index("group")

    def place(rank):
        return (rank // group, lax.rem(rank, group))

    def other(step):
        return place(lax.rem(me + step, ranks))

    left, right = other(ranks - 1), other(1)

    barrier = pltpu.get_barrier_semaphore()

    @pl.loop(1, ranks)
    def _(step):
        pl.semaphore_signal(barrier, inc=1, device_id=other(step), device_id_type=MESH)

    offset = dest_ref[...] - me * cells
    goes_left = offset < 0
    goes_right = offset >= cells
    slot = jnp.where(goes_left, offset + cells, jnp.where(goes_right, offset - cells, offset))
    payload[0:BLOCK, :] = rhs_ref[...]
    payload[KAPPA : KAPPA + 1, :] = cond_ref[...]
    payload[TAG : TAG + 1, :] = (slot + 1).astype(F32)
    payload[TAG + 1 : TAG + 2, :] = jnp.zeros((1, cells), F32)
    parts = jnp.concatenate(split_three(payload[...]), 0)
    row8 = iota((8, cells), 0)
    leaving = jnp.where(
        row8 == 0,
        jnp.where(goes_left, 1.0, 0.0),
        jnp.where(row8 == 1, jnp.where(goes_right, 1.0, 0.0), 0.0),
    ).astype(BF)
    triangle = jnp.where(iota((cells, cells), 0) <= iota((cells, cells), 1), 1.0, 0.0).astype(BF)
    order = dot(leaving, triangle).astype(jnp.int32) - 1
    slots = iota((MOVE, cells), 0)
    pick = jnp.concatenate(
        [
            one_hot(jnp.where(goes_left, order[0:1], -1), slots),
            one_hot(jnp.where(goes_right, order[1:2], -1), slots),
        ],
        0,
    )
    chosen = dot_last(pick, parts)
    chosen = chosen[:, :ROWS] + chosen[:, ROWS : 2 * ROWS] + chosen[:, 2 * ROWS :]
    packed[0] = chosen[:MOVE]
    packed[1] = chosen[MOVE:]

    pl.semaphore_wait(barrier, ranks - 1)

    def exchange(source, target, send_sem, recv_sem):
        copies = [
            pltpu.make_async_remote_copy(
                src_ref=source.at[side],
                dst_ref=target.at[1 - side],
                send_sem=send_sem.at[side],
                recv_sem=recv_sem.at[1 - side],
                device_id=device,
                device_id_type=MESH,
            )
            for side, device in ((0, left), (1, right))
        ]
        return copies

    moves = exchange(packed, moved, move_send, move_recv)
    for copy in moves:
        copy.start()

    stay = one_hot(iota((cells, cells), 0), offset)
    arrived = dot_last(parts, stay)
    cell_rows = iota((cells, cells), 0)
    ghost_rows = iota((ghost, cells), 0)
    for face in range(6):
        local_hot[face] = one_hot(neigh_ref[face : face + 1, :], cell_rows)
    for side in range(2):
        ghost_hot[side] = one_hot(
            neigh_ref[side : side + 1, :] - (cells + side * ghost), ghost_rows
        )
        send_hot[side] = one_hot(list_ref[side : side + 1, :], iota((cells, ghost), 0))

    for copy in moves:
        copy.wait()
    record = moved[...].reshape(2 * MOVE, ROWS)
    landing = record[:, TAG : TAG + 1].astype(jnp.int32) - 1
    record_parts = jnp.concatenate(split_three(record.T), 0)
    arrived = arrived + dot(record_parts, one_hot(landing, iota((2 * MOVE, cells), 1)))
    arrived = arrived[:ROWS] + arrived[ROWS : 2 * ROWS] + arrived[2 * ROWS :]
    rows = iota((ROWS, cells), 0)
    field = jnp.where(rows < BLOCK, arrived, 0.0)
    kappa = arrived[KAPPA : KAPPA + 1]
    cell_weight = column_ref[:, 0:1]
    face_weight = column_ref[0:PART, 1:2]
    first_odd = column_ref[0:PART, 2:3]
    second_odd = column_ref[0:PART, 3:4]

    def operate(field, turn, between):
        high, low = split_two(jnp.where(rows == KAPPA, kappa, field))
        stacked = jnp.concatenate([high, low, high], 0)

        def faces_of(first, last):
            part = dot(forward_ref[first * FACE : last * FACE, :], stacked)
            own, halves = [], []
            for index in range(last - first):
                value = part[index * FACE : index * FACE + PART]
                flux = kappa * part[index * FACE + PART : (index + 1) * FACE]
                own.append((value, flux))
                halves.append(
                    jnp.concatenate(split_two(jnp.concatenate([value, flux], 0)), 0)
                )
            return own, halves

        own, halves = faces_of(0, 2)
        for side in range(2):
            out = dot(halves[side], send_hot[side])
            halo_out[turn, side] = out[:FACE] + out[FACE:]
        copies = exchange(
            halo_out.at[turn], halo_in.at[turn], halo_send.at[turn], halo_recv.at[turn]
        )
        for copy in copies:
            copy.start()
        more_own, more_halves = faces_of(2, 6)
        own, halves = own + more_own, halves + more_halves

        def coefficients(face, near):
            value, flux = own[face]
            code = orient_ref[face : face + 1, :]
            first_bit = jnp.where(lax.rem(code, 2) == 1, 1.0, 0.0)
            second_bit = jnp.where(code >= 2, 1.0, 0.0)
            sign = (1.0 - first_odd * first_bit) * (1.0 - second_odd * second_bit)
            outside = jnp.where(neigh_ref[face : face + 1, :] < 0, 1.0, 0.0)
            near = near[:FACE] + near[FACE:]
            near_kappa = near[FACE_KAPPA : FACE_KAPPA + 1] + outside * kappa
            penalty = PENALTY * jnp.maximum(kappa, near_kappa)
            jump = value - (sign * near[:PART] - outside * value)
            mean = flux - (sign * near[PART:] - outside * flux)
            return [
                face_weight * (penalty * jump - 0.5 * mean),
                face_weight * (-0.5 * kappa * jump),
            ]

        def lifted(terms, first, last):
            high, low = split_two(jnp.concatenate(terms, 0))
            both = dot(backward_ref[:, first * FACE : last * FACE], high)
            rest = dot(backward_ref[0:ROWS, first * FACE : last * FACE], low)
            return both[:ROWS] + both[ROWS:] + rest

        terms = []
        for face in range(2, 6):
            terms += coefficients(face, dot(halves[face ^ 1], local_hot[face]))
        result = lifted(terms, 2, 6)
        stiff = dot(forward_ref[6 * FACE :, :], stacked)
        result = result + cell_weight * field + kappa * stiff
        near = [dot(halves[face ^ 1], local_hot[face]) for face in range(2)]
        between()
        for copy in copies:
            copy.wait()
        terms = []
        for face in range(2):
            received = jnp.concatenate(split_two(halo_in[turn, face]), 0)
            terms += coefficients(face, near[face] + dot(received, ghost_hot[face]))
        return result + lifted(terms, 0, 2)

    def total(value):
        part = jnp.sum(value, 0, keepdims=True)
        return jnp.sum(part, 1, keepdims=True)

    image = operate(field, 0, lambda: None)
    found = []

    def early_sums():
        found.append(total(field * field))
        found.append(total(field * image))
        found.append(total(image * image))

    second = operate(image, 1, early_sums)
    found.append(total(image * second))

    lane = iota((1, ROWS), 1)
    message = jnp.zeros((1, ROWS), F32)
    for index, value in enumerate(found):
        message = jnp.where(lane == index, value, message)
    sums[0] = message

    @pl.loop(1, ranks)
    def _(step):
        pltpu.make_async_remote_copy(
            src_ref=sums.at[0],
            dst_ref=sums.at[step],
            send_sem=sum_send,
            recv_sem=sum_recv,
            device_id=other(step),
            device_id_type=MESH,
        ).start()

    rest = sums.at[pl.ds(1, ranks - 1)]
    pltpu.make_async_copy(rest, rest, sum_send).wait()
    pltpu.make_async_copy(rest, rest, sum_recv).wait()
    summed = jnp.sum(sums[...], 0)
    s00, s01, s11, s12 = (summed[:, index : index + 1] for index in range(4))
    first_step = s00 / s01
    next_norm = s00 - 2.0 * first_step * s01 + first_step * first_step * s11
    inner = s01 - 2.0 * first_step * s11 + first_step * first_step * s12
    beta = next_norm / s00
    second_step = next_norm / (inner - beta * next_norm / first_step)
    linear = first_step + second_step * (1.0 + beta)
    square = first_step * second_step
    field, image, second = field[:BLOCK], image[:BLOCK], second[:BLOCK]
    x_ref[...] = linear * field - square * image
    r_ref[...] = field - linear * image + square * second


def body(shape, right_side, conductivity, destination, neighbour, orientation, send_list):
    cells = right_side.shape[1]
    ghost = send_list.shape[1]
    ranks = shape[0] * shape[1]
    forward, backward, columns = tables()
    vmem = pl.BlockSpec(memory_space=pltpu.VMEM)
    dma = pltpu.SemaphoreType.DMA
    return pl.pallas_call(
        functools.partial(kernel, shape),
        out_shape=(jax.ShapeDtypeStruct((BLOCK, cells), F32),) * 2,
        in_specs=[vmem] * 9,
        out_specs=(vmem, vmem),
        scratch_shapes=[
            pltpu.VMEM((ROWS, cells), F32),
            pltpu.VMEM((6, cells, cells), BF),
            pltpu.VMEM((2, ghost, cells), BF),
            pltpu.VMEM((2, cells, ghost), BF),
            pltpu.VMEM((2, MOVE, ROWS), F32),
            pltpu.VMEM((2, MOVE, ROWS), F32),
            pltpu.VMEM((2, 2, FACE, ghost), F32),
            pltpu.VMEM((2, 2, FACE, ghost), F32),
            pltpu.VMEM((ranks, 1, ROWS), F32),
            dma((2,)),
            dma((2,)),
            dma((2, 2)),
            dma((2, 2)),
            dma,
            dma,
        ],
        compiler_params=pltpu.CompilerParams(collective_id=0, has_side_effects=True),
    )(
        right_side,
        conductivity[None],
        destination[None],
        neighbour,
        orientation,
        send_list,
        jnp.asarray(forward),
        jnp.asarray(backward),
        jnp.asarray(columns),
    )


def solution(mesh):
    both = ("curve", "group")
    shape = (mesh.shape["curve"], mesh.shape["group"])
    in_specs = (P(None, both), P(both), P(both), P(None, both), P(None, both), P(None, both))
    out_specs = (P(None, both), P(None, both))
    return jax.shard_map(
        functools.partial(body, shape),
        mesh=mesh,
        in_specs=in_specs,
        out_specs=out_specs,
        check_vma=False,
    )
```

profile of v0, /device:TPU:0, one launch (start us, length us, event | category | flops | bytes accessed | tf_op | source)
XLA Modules:
  0.0 32.9 jit_solution(6218201131372499544)
XLA Ops:
  0.6 29.9 %shard_map.104 = (f32[125,512]{1,0:T(8,128)}, f32[125,512]{1,0:T(8,128)}) custom-call(f32[125,512]{1,0:T(8,128)} %rhs_ref.1, f32[1,512]{1,0:T(1,128)} %bitcast.2, s32[1,512]{1,0:T(1,128)} %bitcast.3, s32[6,512]{1,0:T(8,128)} %neigh_ref.1, s32[6,512]{1,0:T(8,128)} %orient_ref.1, s32[2,256]{1,0:T(2,128)} %list_ref.1, ...), custom_call_target="tpu_custom_call" | custom-call | tf_op jit(solution)/shard_map/pallas_call | solution.py:402
  30.5 0.0 copy-start
  30.5 1.7 %copy.13 = f32[125,512]{1,0:T(8,128)} copy(f32[125,512]{1,0:T(8,128)} %get-tuple-element.4) | data formatting | bytes 512000
  32.2 0.0 copy-done
  32.2 0.7 %copy.14 = f32[125,512]{1,0:T(8,128)} copy(f32[125,512]{1,0:T(8,128)S(1)} %copy-done) | data formatting | bytes 512000
Async XLA Ops:
  30.5 1.7 %copy-start = (f32[125,512]{1,0:T(8,128)S(1)}, f32[125,512]{1,0:T(8,128)}, u32[]{:S(2)}) copy-start(f32[125,512]{1,0:T(8,128)} %get-tuple-element.5) | copy-start | bytes 768004
where the time goes:
time: 33.1 us; the launch traced here: 32.9 us
  Pallas kernels  29.9 us (90%)
  local copies, waits for them, and re-layouts  2.42 us (7%)
  between operations  0.65 us (2%)
    pallas_call x1, Pallas kernels, body(): pl.pallas_call(functools.partial(kernel, shape), out_shape=(jax.ShapeDtyp...  29.9 us
    unnamed x4, local copies, waits for them, and re-layouts  2.42 us

commit v1 on v0

--- a/solution.py
+++ b/solution.py
@@ -22,6 +22,7 @@
 PART = 32
 FACE = 2 * PART
 FACE_KAPPA = 25
+FACE_TAG = 26
 
 GAUSS_POINTS = (-0.906179845938664, -0.5384693101056831, 0.0, 0.5384693101056831, 0.906179845938664)
 GAUSS_WEIGHTS = (
@@ -152,6 +153,17 @@
 
 def kernel(
     shape,
+    rhs_hbm,
+    cond_hbm,
+    dest_hbm,
+    neigh_hbm,
+    orient_hbm,
+    list_hbm,
+    forward_hbm,
+    backward_hbm,
+    column_hbm,
+    basis_hbm,
+    step_ref,
     rhs_ref,
     cond_ref,
     dest_ref,
@@ -161,19 +173,24 @@
     forward_ref,
     backward_ref,
     column_ref,
-    x_ref,
-    r_ref,
+    basis,
     payload,
     local_hot,
     ghost_hot,
     send_hot,
     packed,
     moved,
+    far_out,
+    far_in,
     halo_out,
     halo_in,
     sums,
+    load_sem,
+    store_sem,
     move_send,
     move_recv,
+    far_send,
+    far_recv,
     halo_send,
     halo_recv,
     sum_send,
@@ -191,13 +208,42 @@
     def other(step):
         return place(lax.rem(me + step, ranks))
 
-    left, right = other(ranks - 1), other(1)
-
     barrier = pltpu.get_barrier_semaphore()
 
     @pl.loop(1, ranks)
     def _(step):
         pl.semaphore_signal(barrier, inc=1, device_id=other(step), device_id_type=MESH)
+
+    loads = [
+        pltpu.make_async_copy(source, target, load_sem.at[index])
+        for index, (source, target) in enumerate(
+            (
+                (dest_hbm, dest_ref),
+                (list_hbm, list_ref),
+                (cond_hbm, cond_ref),
+                (rhs_hbm, rhs_ref),
+                (forward_hbm, forward_ref),
+                (neigh_hbm, neigh_ref),
+                (orient_hbm, orient_ref),
+                (column_hbm, column_ref),
+                (backward_hbm, backward_ref),
+            )
+        )
+    ]
+    for load in loads:
+        load.start()
+    for load in loads:
+        load.wait()
+
+    def faces_of(stacked, kappa, first, last):
+        part = dot(forward_ref[first * FACE : last * FACE, :], stacked)
+        own, halves = [], []
+        for index in range(last - first):
+            value = part[index * FACE : index * FACE + PART]
+            flux = kappa * part[index * FACE + PART : (index + 1) * FACE]
+            own.append((value, flux))
+            halves.append(jnp.concatenate(split_two(jnp.concatenate([value, flux], 0)), 0))
+        return own, halves
 
     offset = dest_ref[...] - me * cells
     goes_left = offset < 0
@@ -207,7 +253,8 @@
     payload[KAPPA : KAPPA + 1, :] = cond_ref[...]
     payload[TAG : TAG + 1, :] = (slot + 1).astype(F32)
     payload[TAG + 1 : TAG + 2, :] = jnp.zeros((1, cells), F32)
-    parts = jnp.concatenate(split_three(payload[...]), 0)
+    high, mid, low = split_three(payload[...])
+    parts = jnp.concatenate([high, mid, low], 0)
     row8 = iota((8, cells), 0)
     leaving = jnp.where(
         row8 == 0,
@@ -229,10 +276,27 @@
     packed[0] = chosen[:MOVE]
     packed[1] = chosen[MOVE:]
 
+    old_halves = faces_of(jnp.concatenate([high, mid, high], 0), cond_ref[...], 0, 2)[1]
+    offset_column = jnp.broadcast_to(offset.astype(F32), (8, cells)).T[:, 0:1]
+    lists = list_ref[...].astype(F32)
+    face_rows = iota((FACE, ghost), 0)
+    for side in range(2):
+        hot = one_hot(offset_column, lists[side : side + 1, :])
+        out = dot(old_halves[side], hot)
+        halo_out[0, side] = jnp.where(
+            face_rows == FACE_TAG, lists[side : side + 1, :], out[:FACE] + out[FACE:]
+        )
+    lanes = iota((2 * MOVE, ROWS), 1)
+    tagged = jnp.where(lanes == FACE_TAG, chosen[:, TAG : TAG + 1], 0.0)
+    leaving_low = dot_last(pick, old_halves[0]) + tagged
+    leaving_high = dot_last(pick, old_halves[1]) + tagged
+    far_out[0] = leaving_low[:MOVE]
+    far_out[1] = leaving_high[MOVE:]
+
     pl.semaphore_wait(barrier, ranks - 1)
 
-    def exchange(source, target, send_sem, recv_sem):
-        copies = [
+    def exchange(source, target, send_sem, recv_sem, reach):
+        return [
             pltpu.make_async_remote_copy(
                 src_ref=source.at[side],
                 dst_ref=target.at[1 - side],
@@ -241,12 +305,13 @@
                 device_id=device,
                 device_id_type=MESH,
             )
-            for side, device in ((0, left), (1, right))
+            for side, device in ((0, other(ranks - reach)), (1, other(reach)))
         ]
-        return copies
-
-    moves = exchange(packed, moved, move_send, move_recv)
-    for copy in moves:
+
+    moves = exchange(packed, moved, move_send, move_recv, 1)
+    halos = exchange(halo_out.at[0], halo_in.at[0], halo_send.at[0], halo_recv.at[0], 1)
+    fars = exchange(far_out, far_in, far_send, far_recv, 2)
+    for copy in moves + fars + halos:
         copy.start()
 
     stay = one_hot(iota((cells, cells), 0), offset)
@@ -279,29 +344,18 @@
     def operate(field, turn, between):
         high, low = split_two(jnp.where(rows == KAPPA, kappa, field))
         stacked = jnp.concatenate([high, low, high], 0)
-
-        def faces_of(first, last):
-            part = dot(forward_ref[first * FACE : last * FACE, :], stacked)
-            own, halves = [], []
-            for index in range(last - first):
-                value = part[index * FACE : index * FACE + PART]
-                flux = kappa * part[index * FACE + PART : (index + 1) * FACE]
-                own.append((value, flux))
-                halves.append(
-                    jnp.concatenate(split_two(jnp.concatenate([value, flux], 0)), 0)
-                )
-            return own, halves
-
-        own, halves = faces_of(0, 2)
-        for side in range(2):
-            out = dot(halves[side], send_hot[side])
-            halo_out[turn, side] = out[:FACE] + out[FACE:]
-        copies = exchange(
-            halo_out.at[turn], halo_in.at[turn], halo_send.at[turn], halo_recv.at[turn]
-        )
-        for copy in copies:
-            copy.start()
-        more_own, more_halves = faces_of(2, 6)
+        own, halves = faces_of(stacked, kappa, 0, 2)
+        copies = halos + fars
+        if turn:
+            for side in range(2):
+                out = dot(halves[side], send_hot[side])
+                halo_out[turn, side] = out[:FACE] + out[FACE:]
+            copies = exchange(
+                halo_out.at[turn], halo_in.at[turn], halo_send.at[turn], halo_recv.at[turn], 1
+            )
+            for copy in copies:
+                copy.start()
+        more_own, more_halves = faces_of(stacked, kappa, 2, 6)
         own, halves = own + more_own, halves + more_halves
 
         def coefficients(face, near):
@@ -316,10 +370,8 @@
             penalty = PENALTY * jnp.maximum(kappa, near_kappa)
             jump = value - (sign * near[:PART] - outside * value)
             mean = flux - (sign * near[PART:] - outside * flux)
-            return [
-                face_weight * (penalty * jump - 0.5 * mean),
-                face_weight * (-0.5 * kappa * jump),
-            ]
+            scaled = -0.5 * (face_weight * jump)
+            return face_weight * (penalty * jump - 0.5 * mean), kappa * scaled, scaled
 
         def lifted(terms, first, last):
             high, low = split_two(jnp.concatenate(terms, 0))
@@ -329,39 +381,57 @@
 
         terms = []
         for face in range(2, 6):
-            terms += coefficients(face, dot(halves[face ^ 1], local_hot[face]))
+            terms += coefficients(face, dot(halves[face ^ 1], local_hot[face]))[:2]
         result = lifted(terms, 2, 6)
         stiff = dot(forward_ref[6 * FACE :, :], stacked)
         result = result + cell_weight * field + kappa * stiff
         near = [dot(halves[face ^ 1], local_hot[face]) for face in range(2)]
-        between()
+        between(result)
         for copy in copies:
             copy.wait()
-        terms = []
+        terms, energy = [], 0.0
         for face in range(2):
-            received = jnp.concatenate(split_two(halo_in[turn, face]), 0)
-            terms += coefficients(face, near[face] + dot(received, ghost_hot[face]))
-        return result + lifted(terms, 0, 2)
-
-    def total(value):
-        part = jnp.sum(value, 0, keepdims=True)
-        return jnp.sum(part, 1, keepdims=True)
-
-    image = operate(field, 0, lambda: None)
+            ghosts = halo_in[turn, face]
+            if not turn:
+                gone = leaving_high[:MOVE] if face == 0 else leaving_low[MOVE:]
+                wide = jnp.concatenate([far_in[face], gone], 0)
+                hot = one_hot(wide[:, FACE_TAG : FACE_TAG + 1] - 1.0, ghosts[FACE_TAG : FACE_TAG + 1])
+                placed = dot(wide.T.astype(BF), hot)
+                ghosts = ghosts + placed[:FACE] + placed[FACE:]
+            received = jnp.concatenate(split_two(ghosts), 0)
+            first, second, scaled = coefficients(face, near[face] + dot(received, ghost_hot[face]))
+            terms += [first, second]
+            energy = energy + jnp.sum(own[face][0] * first + own[face][1] * scaled, 0, keepdims=True)
+        return result, energy, lambda: lifted(terms, 0, 2)
+
+    def down(value):
+        return jnp.sum(value, 0, keepdims=True)
+
+    def save(index, value):
+        basis[index] = value
+        return pltpu.make_async_copy(basis.at[index], basis_hbm.at[index], store_sem.at[index])
+
+    stores = [save(0, field)]
+    stores[0].start()
+    result, _, lift = operate(field, 0, lambda result: None)
+    image = result + lift()
+    stores.append(save(1, image))
+    stores[1].start()
     found = []
 
-    def early_sums():
-        found.append(total(field * field))
-        found.append(total(field * image))
-        found.append(total(image * image))
-
-    second = operate(image, 1, early_sums)
-    found.append(total(image * second))
+    def early_sums(result):
+        found.append(down(field * field))
+        found.append(down(field * image))
+        found.append(down(image * image))
+        found.append(down(image * result))
+
+    result, energy, lift = operate(image, 1, early_sums)
+    found[3] = found[3] + energy
 
     lane = iota((1, ROWS), 1)
     message = jnp.zeros((1, ROWS), F32)
     for index, value in enumerate(found):
-        message = jnp.where(lane == index, value, message)
+        message = jnp.where(lane == index, jnp.sum(value, 1, keepdims=True), message)
     sums[0] = message
 
     @pl.loop(1, ranks)
@@ -375,6 +445,8 @@
             device_id_type=MESH,
         ).start()
 
+    stores.append(save(2, result + lift()))
+    stores[2].start()
     rest = sums.at[pl.ds(1, ranks - 1)]
     pltpu.make_async_copy(rest, rest, sum_send).wait()
     pltpu.make_async_copy(rest, rest, sum_recv).wait()
@@ -387,9 +459,9 @@
     second_step = next_norm / (inner - beta * next_norm / first_step)
     linear = first_step + second_step * (1.0 + beta)
     square = first_step * second_step
-    field, image, second = field[:BLOCK], image[:BLOCK], second[:BLOCK]
-    x_ref[...] = linear * field - square * image
-    r_ref[...] = field - linear * image + square * second
+    step_ref[...] = jnp.where(iota(step_ref.shape, 0) == 0, linear, square)
+    for store in stores:
+        store.wait()
 
 
 def body(shape, right_side, conductivity, destination, neighbour, orientation, send_list):
@@ -398,31 +470,9 @@
     ranks = shape[0] * shape[1]
     forward, backward, columns = tables()
     vmem = pl.BlockSpec(memory_space=pltpu.VMEM)
+    anywhere = pl.BlockSpec(memory_space=pl.ANY)
     dma = pltpu.SemaphoreType.DMA
-    return pl.pallas_call(
-        functools.partial(kernel, shape),
-        out_shape=(jax.ShapeDtypeStruct((BLOCK, cells), F32),) * 2,
-        in_specs=[vmem] * 9,
-        out_specs=(vmem, vmem),
-        scratch_shapes=[
-            pltpu.VMEM((ROWS, cells), F32),
-            pltpu.VMEM((6, cells, cells), BF),
-            pltpu.VMEM((2, ghost, cells), BF),
-            pltpu.VMEM((2, cells, ghost), BF),
-            pltpu.VMEM((2, MOVE, ROWS), F32),
-            pltpu.VMEM((2, MOVE, ROWS), F32),
-            pltpu.VMEM((2, 2, FACE, ghost), F32),
-            pltpu.VMEM((2, 2, FACE, ghost), F32),
-            pltpu.VMEM((ranks, 1, ROWS), F32),
-            dma((2,)),
-            dma((2,)),
-            dma((2, 2)),
-            dma((2, 2)),
-            dma,
-            dma,
-        ],
-        compiler_params=pltpu.CompilerParams(collective_id=0, has_side_effects=True),
-    )(
+    operands = (
         right_side,
         conductivity[None],
         destination[None],
@@ -433,6 +483,44 @@
         jnp.asarray(backward),
         jnp.asarray(columns),
     )
+    basis, steps = pl.pallas_call(
+        functools.partial(kernel, shape),
+        out_shape=(
+            jax.ShapeDtypeStruct((3, ROWS, cells), F32),
+            jax.ShapeDtypeStruct((2, cells), F32),
+        ),
+        in_specs=[anywhere] * len(operands),
+        out_specs=(anywhere, vmem),
+        scratch_shapes=[pltpu.VMEM(item.shape, item.dtype) for item in operands]
+        + [
+            pltpu.VMEM((3, ROWS, cells), F32),
+            pltpu.VMEM((ROWS, cells), F32),
+            pltpu.VMEM((6, cells, cells), BF),
+            pltpu.VMEM((2, ghost, cells), BF),
+            pltpu.VMEM((2, cells, ghost), BF),
+            pltpu.VMEM((2, MOVE, ROWS), F32),
+            pltpu.VMEM((2, MOVE, ROWS), F32),
+            pltpu.VMEM((2, MOVE, ROWS), F32),
+            pltpu.VMEM((2, MOVE, ROWS), F32),
+            pltpu.VMEM((2, 2, FACE, ghost), F32),
+            pltpu.VMEM((2, 2, FACE, ghost), F32),
+            pltpu.VMEM((ranks, 1, ROWS), F32),
+            dma((len(operands),)),
+            dma((3,)),
+            dma((2,)),
+            dma((2,)),
+            dma((2,)),
+            dma((2,)),
+            dma((2, 2)),
+            dma((2, 2)),
+            dma,
+            dma,
+        ],
+        compiler_params=pltpu.CompilerParams(collective_id=0, has_side_effects=True),
+    )(*operands)
+    linear, square = steps[0:1], steps[1:2]
+    first, second, third = (basis[index, :BLOCK] for index in range(3))
+    return linear * first - square * second, first - linear * second + square * third
 
 
 def solution(mesh):

time: 33.1 us -> 28.9 us (0.87)
  Pallas kernels: 29.9 us -> 25.3 us
  other arithmetic: 0 us -> 1.99 us
  local copies, waits for them, and re-layouts: 2.42 us -> 0.76 us
    pallas_call x1, Pallas kernels: 29.9 us -> 25.3 us  [body(): pl.pallas_call(functools.partial(kernel, shape), out_shape=(jax.ShapeDtyp...]
    unnamed x4 -> x0, local copies, waits for them, and re-layouts: 2.42 us -> none
    add x0 -> x1, other arithmetic: none -> 1.99 us  [body(): first - linear * second + square * third]
    slice x0 -> x1, local copies, waits for them, and re-layouts: none -> 0.76 us  [body(): linear, square = (steps[0:1], steps[1:2])]
where the time goes in v1:
time: 28.9 us; the launch traced here: 28.7 us
  Pallas kernels  25.3 us (88%)
  other arithmetic  1.99 us (7%)
  local copies, waits for them, and re-layouts  0.76 us (3%)
  between operations  0.64 us (2%)
    pallas_call x1, Pallas kernels, body(): pl.pallas_call(functools.partial(kernel, shape), out_shape=(jax.ShapeDtyp...  25.3 us
    add x1, other arithmetic, body(): first - linear * second + square * third  1.99 us
    slice x1, local copies, waits for them, and re-layouts, body(): linear, square = (steps[0:1], steps[1:2])  0.76 us

profile of v1, /device:TPU:0, one launch (start us, length us, event | category | flops | bytes accessed | tf_op | source)
XLA Modules:
  0.0 28.7 jit_solution(13115367903003268431)
XLA Ops:
  0.6 25.3 %shard_map.104 = (f32[3,128,512]{2,1,0:T(8,128)}, f32[2,512]{1,0:T(2,128)}) custom-call(f32[125,512]{1,0:T(8,128)} %rhs_hbm.1, f32[1,512]{1,0:T(1,128)} %bitcast.24, s32[1,512]{1,0:T(1,128)} %bitcast.25, s32[6,512]{1,0:T(8,128)} %neigh_hbm.1, s32[6,512]{1,0:T(8,128)} %orient_hbm.1, s32[2,256]{1,0:T(2,128)} %list_hbm.1, ...), custom_call_target="tpu_custom_call" | custom-call | tf_op jit(solution)/shard_map/pallas_call | solution.py:486
  26.0 0.8 %fusion.3 = (f32[1,512]{1,0:T(1,128)S(1)}, f32[1,512]{1,0:T(1,128)S(1)}) fusion(f32[2,512]{1,0:T(2,128)} %get-tuple-element.4), kind=kLoop, calls=%fused_computation.7 | loop fusion | bytes 8192 | tf_op jit(solution)/shard_map/slice | solution.py:521
  26.7 2.0 %fusion = (f32[125,512]{1,0:T(8,128)}, f32[125,512]{1,0:T(8,128)}) fusion(f32[3,128,512]{2,1,0:T(8,128)} %get-tuple-element.5, f32[512]{0:T(512)S(1)} %bitcast.23, f32[512]{0:T(512)S(1)} %bitcast.22), kind=kLoop, calls=%fused_computation.1 | loop fusion | flops 448000 | bytes 1284096 | tf_op jit(solution)/shard_map/add | solution.py:523

commit v2 on v1

--- a/solution.py
+++ b/solution.py
@@ -11,6 +11,7 @@
 NODES = 5
 BLOCK = 125
 MOVE = 64
+VMEM_LIMIT = 24 * 1024 * 1024
 PENALTY = 80.0
 MESH = pl.DeviceIdType.MESH
 BF = jnp.bfloat16
@@ -163,7 +164,8 @@
     backward_hbm,
     column_hbm,
     basis_hbm,
-    step_ref,
+    linear_ref,
+    square_ref,
     rhs_ref,
     cond_ref,
     dest_ref,
@@ -459,7 +461,8 @@
     second_step = next_norm / (inner - beta * next_norm / first_step)
     linear = first_step + second_step * (1.0 + beta)
     square = first_step * second_step
-    step_ref[...] = jnp.where(iota(step_ref.shape, 0) == 0, linear, square)
+    linear_ref[...] = jnp.broadcast_to(linear, (1, cells))
+    square_ref[...] = jnp.broadcast_to(square, (1, cells))
     for store in stores:
         store.wait()
 
@@ -483,14 +486,15 @@
         jnp.asarray(backward),
         jnp.asarray(columns),
     )
-    basis, steps = pl.pallas_call(
+    basis, linear, square = pl.pallas_call(
         functools.partial(kernel, shape),
         out_shape=(
             jax.ShapeDtypeStruct((3, ROWS, cells), F32),
-            jax.ShapeDtypeStruct((2, cells), F32),
+            jax.ShapeDtypeStruct((1, cells), F32),
+            jax.ShapeDtypeStruct((1, cells), F32),
         ),
-        in_specs=[anywhere] * len(operands),
-        out_specs=(anywhere, vmem),
+        in_specs=[pl.BlockSpec(memory_space=pltpu.HBM)] * len(operands),
+        out_specs=(anywhere, vmem, vmem),
         scratch_shapes=[pltpu.VMEM(item.shape, item.dtype) for item in operands]
         + [
             pltpu.VMEM((3, ROWS, cells), F32),
@@ -516,9 +520,10 @@
             dma,
             dma,
         ],
-        compiler_params=pltpu.CompilerParams(collective_id=0, has_side_effects=True),
+        compiler_params=pltpu.CompilerParams(
+            collective_id=0, has_side_effects=True, vmem_limit_bytes=VMEM_LIMIT
+        ),
     )(*operands)
-    linear, square = steps[0:1], steps[1:2]
     first, second, third = (basis[index, :BLOCK] for index in range(3))
     return linear * first - square * second, first - linear * second + square * third
 

time: 28.9 us -> 33.3 us (1.15)
  local copies, waits for them, and re-layouts: 0.76 us -> 7.18 us
  Pallas kernels: 25.3 us -> 24.1 us
  other arithmetic: 1.99 us -> 0.88 us
    unnamed x0 -> x18, local copies, waits for them, and re-layouts: none -> 7.18 us
    pallas_call x1, Pallas kernels: 25.3 us -> 24.1 us  [body(): pl.pallas_call(functools.partial(kernel, shape), out_shape=(jax.ShapeDtyp...]
    add x1, other arithmetic: 1.99 us -> 0.88 us  [body(): first - linear * second + square * third]
    slice x1 -> x0, local copies, waits for them, and re-layouts: 0.76 us -> none  [body(): linear, square = (steps[0:1], steps[1:2])]
where the time goes in v2:
time: 33.3 us; the launch traced here: 32.8 us
  Pallas kernels  24.1 us (72%)
  local copies, waits for them, and re-layouts  7.18 us (22%)
  other arithmetic  0.88 us (3%)
  between operations  0.66 us (2%)
    pallas_call x1, Pallas kernels, body(): pl.pallas_call(functools.partial(kernel, shape), out_shape=(jax.ShapeDtyp...  24.1 us
    unnamed x18, local copies, waits for them, and re-layouts  7.18 us
    add x1, other arithmetic, body(): first - linear * second + square * third  0.88 us

profile of v2, /device:TPU:0, one launch (start us, length us, event | category | flops | bytes accessed | tf_op | source)
XLA Modules:
  0.0 32.8 jit_solution(13082560578877791736)
XLA Ops:
  0.6 0.0 copy-start.6
  0.6 0.7 %copy-done.6 = f32[512]{0:T(512)S(1)} copy-done((f32[512]{0:T(512)S(1)}, f32[512]{0:T(512)}, u32[]{:S(2)}) %copy-start.6) | copy-done | bytes 2072
  1.3 0.0 copy-start
  1.3 1.0 %copy-done = bf16[512,384]{1,0:T(8,128)(2,1)S(1)} copy-done((bf16[512,384]{1,0:T(8,128)(2,1)S(1)}, bf16[512,384]{1,0:T(8,128)(2,1)}, u32[]{:S(2)}) %copy-start) | copy-done | bytes 393240
  2.3 0.0 copy-start.1
  2.3 0.9 %copy-done.1 = f32[125,512]{1,0:T(8,128)S(1)} copy-done((f32[125,512]{1,0:T(8,128)S(1)}, f32[125,512]{1,0:T(8,128)}, u32[]{:S(2)}) %copy-start.1) | copy-done | bytes 256024
  3.3 0.0 copy-start.2
  3.3 0.9 %copy-done.2 = bf16[256,384]{1,0:T(8,128)(2,1)S(1)} copy-done((bf16[256,384]{1,0:T(8,128)(2,1)S(1)}, bf16[256,384]{1,0:T(8,128)(2,1)}, u32[]{:S(2)}) %copy-start.2) | copy-done | bytes 196632
  4.2 0.0 copy-start.3
  4.2 0.8 %copy-done.3 = f32[128,128]{1,0:T(8,128)S(1)} copy-done((f32[128,128]{1,0:T(8,128)S(1)}, f32[128,128]{1,0:T(8,128)}, u32[]{:S(2)}) %copy-start.3) | copy-done | bytes 65560
  5.0 0.0 copy-start.4
  5.0 0.7 %copy-done.4 = s32[6,512]{1,0:T(8,128)S(1)} copy-done((s32[6,512]{1,0:T(8,128)S(1)}, s32[6,512]{1,0:T(8,128)}, u32[]{:S(2)}) %copy-start.4) | copy-done | bytes 12312
  5.7 0.0 copy-start.5
  5.7 0.7 %copy-done.5 = s32[6,512]{1,0:T(8,128)S(1)} copy-done((s32[6,512]{1,0:T(8,128)S(1)}, s32[6,512]{1,0:T(8,128)}, u32[]{:S(2)}) %copy-start.5) | copy-done | bytes 12312
  6.5 0.0 copy-start.7
  6.5 0.7 %copy-done.7 = s32[512]{0:T(512)S(1)} copy-done((s32[512]{0:T(512)S(1)}, s32[512]{0:T(512)}, u32[]{:S(2)}) %copy-start.7) | copy-done | bytes 2072
  7.1 0.0 copy-start.8
  7.1 0.7 %copy-done.8 = s32[2,256]{1,0:T(2,128)S(1)} copy-done((s32[2,256]{1,0:T(2,128)S(1)}, s32[2,256]{1,0:T(2,128)}, u32[]{:S(2)}) %copy-start.8) | copy-done | bytes 2072
  7.8 24.1 %shard_map.104 = (f32[3,128,512]{2,1,0:T(8,128)S(1)}, f32[1,512]{1,0:T(1,128)S(1)}, f32[1,512]{1,0:T(1,128)S(1)}) custom-call(f32[125,512]{1,0:T(8,128)S(1)} %copy-done.1, f32[1,512]{1,0:T(1,128)S(1)} %bitcast.22, s32[1,512]{1,0:T(1,128)S(1)} %bitcast.23, s32[6,512]{1,0:T(8,128)S(1)} %copy-done.4, s32[6,512]{1,0:T(8,128)S(1)} %copy-done.5, ...), custom_call_target="tpu_custom_call" | custom-call | tf_op jit(solution)/shard_map/pallas_call | solution.py:489
  31.9 0.9 %fusion = (f32[125,512]{1,0:T(8,128)}, f32[125,512]{1,0:T(8,128)}) fusion(f32[3,128,512]{2,1,0:T(8,128)S(1)} %get-tuple-element.6, f32[512]{0:T(512)S(1)} %bitcast.25, f32[512]{0:T(512)S(1)} %bitcast.24), kind=kLoop, calls=%fused_computation.1 | loop fusion | flops 448000 | bytes 1284096 | tf_op jit(solution)/shard_map/add | solution.py:528
Async XLA Ops:
  0.6 0.7 %copy-start.6 = (f32[512]{0:T(512)S(1)}, f32[512]{0:T(512)}, u32[]{:S(2)}) copy-start(f32[512]{0:T(512)} %param.10) | copy-start | bytes 6148
  1.3 1.0 %copy-start = (bf16[512,384]{1,0:T(8,128)(2,1)S(1)}, bf16[512,384]{1,0:T(8,128)(2,1)}, u32[]{:S(2)}) copy-start(bf16[512,384]{1,0:T(8,128)(2,1)} %constant.6.clone.forward_hbm) | copy-start | bytes 1179652
  2.3 0.9 %copy-start.1 = (f32[125,512]{1,0:T(8,128)S(1)}, f32[125,512]{1,0:T(8,128)}, u32[]{:S(2)}) copy-start(f32[125,512]{1,0:T(8,128)} %rhs_hbm.1) | copy-start | bytes 768004
  3.3 0.9 %copy-start.2 = (bf16[256,384]{1,0:T(8,128)(2,1)S(1)}, bf16[256,384]{1,0:T(8,128)(2,1)}, u32[]{:S(2)}) copy-start(bf16[256,384]{1,0:T(8,128)(2,1)} %constant.7.clone.backward_hbm) | copy-start | bytes 589828
  4.2 0.8 %copy-start.3 = (f32[128,128]{1,0:T(8,128)S(1)}, f32[128,128]{1,0:T(8,128)}, u32[]{:S(2)}) copy-start(f32[128,128]{1,0:T(8,128)} %constant.8.clone.column_hbm) | copy-start | bytes 196612
  5.0 0.7 %copy-start.4 = (s32[6,512]{1,0:T(8,128)S(1)}, s32[6,512]{1,0:T(8,128)}, u32[]{:S(2)}) copy-start(s32[6,512]{1,0:T(8,128)} %neigh_hbm.1) | copy-start | bytes 36868
  5.7 0.7 %copy-start.5 = (s32[6,512]{1,0:T(8,128)S(1)}, s32[6,512]{1,0:T(8,128)}, u32[]{:S(2)}) copy-start(s32[6,512]{1,0:T(8,128)} %orient_hbm.1) | copy-start | bytes 36868
  6.5 0.7 %copy-start.7 = (s32[512]{0:T(512)S(1)}, s32[512]{0:T(512)}, u32[]{:S(2)}) copy-start(s32[512]{0:T(512)} %param.11) | copy-start | bytes 6148
  7.1 0.7 %copy-start.8 = (s32[2,256]{1,0:T(2,128)S(1)}, s32[2,256]{1,0:T(2,128)}, u32[]{:S(2)}) copy-start(s32[2,256]{1,0:T(2,128)} %list_hbm.1) | copy-start | bytes 6148

commit v3 on v2

--- a/solution.py
+++ b/solution.py
@@ -11,6 +11,7 @@
 NODES = 5
 BLOCK = 125
 MOVE = 64
+UNROLLED = 64
 VMEM_LIMIT = 24 * 1024 * 1024
 PENALTY = 80.0
 MESH = pl.DeviceIdType.MESH
@@ -24,6 +25,8 @@
 FACE = 2 * PART
 FACE_KAPPA = 25
 FACE_TAG = 26
+HALO = PART + 24
+FACE_LAST = 27
 
 GAUSS_POINTS = (-0.906179845938664, -0.5384693101056831, 0.0, 0.5384693101056831, 0.906179845938664)
 GAUSS_WEIGHTS = (
@@ -212,9 +215,29 @@
 
     barrier = pltpu.get_barrier_semaphore()
 
-    @pl.loop(1, ranks)
-    def _(step):
-        pl.semaphore_signal(barrier, inc=1, device_id=other(step), device_id_type=MESH)
+    my_curve, my_group = lax.axis_index("curve"), lax.axis_index("group")
+
+    def for_each_other(act):
+        def order(count):
+            return sorted(range(count), key=lambda step: -min(step, count - step))
+
+        for curve_step in order(curve):
+            to_curve = lax.rem(my_curve + curve_step, curve)
+
+            def one(group_step):
+                to_group = lax.rem(my_group + group_step, group)
+                act(curve_step * group + group_step, (to_curve, to_group))
+
+            if ranks <= UNROLLED:
+                for group_step in order(group):
+                    if curve_step or group_step:
+                        one(group_step)
+            else:
+                pl.loop(0 if curve_step else 1, group)(one)
+
+    for_each_other(
+        lambda _, device: pl.semaphore_signal(barrier, inc=1, device_id=device, device_id_type=MESH)
+    )
 
     loads = [
         pltpu.make_async_copy(source, target, load_sem.at[index])
@@ -234,7 +257,7 @@
     ]
     for load in loads:
         load.start()
-    for load in loads:
+    for load in loads[:4]:
         load.wait()
 
     def faces_of(stacked, kappa, first, last):
@@ -278,15 +301,28 @@
     packed[0] = chosen[:MOVE]
     packed[1] = chosen[MOVE:]
 
+    for load in loads[4:]:
+        load.wait()
+
     old_halves = faces_of(jnp.concatenate([high, mid, high], 0), cond_ref[...], 0, 2)[1]
     offset_column = jnp.broadcast_to(offset.astype(F32), (8, cells)).T[:, 0:1]
     lists = list_ref[...].astype(F32)
-    face_rows = iota((FACE, ghost), 0)
+    halo_rows = iota((HALO, ghost), 0)
+
+    def shrink(out):
+        out = out[:FACE] + out[FACE:]
+        return jnp.where(halo_rows == FACE_LAST, out[HALO : HALO + 1], out[:HALO])
+
+    def widen(message):
+        last = message[FACE_LAST : FACE_LAST + 1]
+        rest = jnp.where(iota((FACE - HALO, ghost), 0) == 0, last, 0.0)
+        return jnp.concatenate([message, rest], 0)
+
     for side in range(2):
         hot = one_hot(offset_column, lists[side : side + 1, :])
         out = dot(old_halves[side], hot)
         halo_out[0, side] = jnp.where(
-            face_rows == FACE_TAG, lists[side : side + 1, :], out[:FACE] + out[FACE:]
+            halo_rows == FACE_TAG, lists[side : side + 1, :], shrink(out)
         )
     lanes = iota((2 * MOVE, ROWS), 1)
     tagged = jnp.where(lanes == FACE_TAG, chosen[:, TAG : TAG + 1], 0.0)
@@ -351,7 +387,7 @@
         if turn:
             for side in range(2):
                 out = dot(halves[side], send_hot[side])
-                halo_out[turn, side] = out[:FACE] + out[FACE:]
+                halo_out[turn, side] = shrink(out)
             copies = exchange(
                 halo_out.at[turn], halo_in.at[turn], halo_send.at[turn], halo_recv.at[turn], 1
             )
@@ -393,7 +429,7 @@
             copy.wait()
         terms, energy = [], 0.0
         for face in range(2):
-            ghosts = halo_in[turn, face]
+            ghosts = widen(halo_in[turn, face])
             if not turn:
                 gone = leaving_high[:MOVE] if face == 0 else leaving_low[MOVE:]
                 wide = jnp.concatenate([far_in[face], gone], 0)
@@ -436,16 +472,16 @@
         message = jnp.where(lane == index, jnp.sum(value, 1, keepdims=True), message)
     sums[0] = message
 
-    @pl.loop(1, ranks)
-    def _(step):
-        pltpu.make_async_remote_copy(
+    for_each_other(
+        lambda index, device: pltpu.make_async_remote_copy(
             src_ref=sums.at[0],
-            dst_ref=sums.at[step],
+            dst_ref=sums.at[index],
             send_sem=sum_send,
             recv_sem=sum_recv,
-            device_id=other(step),
+            device_id=device,
             device_id_type=MESH,
         ).start()
+    )
 
     stores.append(save(2, result + lift()))
     stores[2].start()
@@ -486,6 +522,7 @@
         jnp.asarray(backward),
         jnp.asarray(columns),
     )
+    operands = tuple(pltpu.with_memory_space_constraint(item, pltpu.HBM) for item in operands)
     basis, linear, square = pl.pallas_call(
         functools.partial(kernel, shape),
         out_shape=(
@@ -506,8 +543,8 @@
             pltpu.VMEM((2, MOVE, ROWS), F32),
             pltpu.VMEM((2, MOVE, ROWS), F32),
             pltpu.VMEM((2, MOVE, ROWS), F32),
-            pltpu.VMEM((2, 2, FACE, ghost), F32),
-            pltpu.VMEM((2, 2, FACE, ghost), F32),
+            pltpu.VMEM((2, 2, HALO, ghost), F32),
+            pltpu.VMEM((2, 2, HALO, ghost), F32),
             pltpu.VMEM((ranks, 1, ROWS), F32),
             dma((len(operands),)),
             dma((3,)),

time: 33.3 us -> 25.9 us (0.78)
  local copies, waits for them, and re-layouts: 7.18 us -> 0 us
    unnamed x18 -> x0, local copies, waits for them, and re-layouts: 7.18 us -> none
where the time goes in v3:
time: 25.9 us; the launch traced here: 25.7 us
  Pallas kernels  24.2 us (93%)
  other arithmetic  0.88 us (3%)
  between operations  0.64 us (2%)
    pallas_call x1, Pallas kernels, body(): pl.pallas_call(functools.partial(kernel, shape), out_shape=(jax.ShapeDtyp...  24.2 us
    add x1, other arithmetic, body(): first - linear * second + square * third  0.88 us

profile of v3, /device:TPU:0, one launch (start us, length us, event | category | flops | bytes accessed | tf_op | source)
XLA Modules:
  0.0 25.7 jit_solution(4975917189055209786)
XLA Ops:
  0.6 24.2 %shard_map.104 = (f32[3,128,512]{2,1,0:T(8,128)S(1)}, f32[1,512]{1,0:T(1,128)S(1)}, f32[1,512]{1,0:T(1,128)S(1)}) custom-call(f32[125,512]{1,0:T(8,128)} %rhs_hbm.1, f32[1,512]{1,0:T(1,128)} %bitcast.24, s32[1,512]{1,0:T(1,128)} %bitcast.25, s32[6,512]{1,0:T(8,128)} %neigh_hbm.1, s32[6,512]{1,0:T(8,128)} %orient_hbm.1, s32[2,256]{1,0:T(2,128)} %list_hbm.1, ...), custom_call_target="tpu_custom_call" | custom-call | tf_op jit(solution)/shard_map/pallas_call | solution.py:526
  24.8 0.9 %fusion = (f32[125,512]{1,0:T(8,128)}, f32[125,512]{1,0:T(8,128)}) fusion(f32[3,128,512]{2,1,0:T(8,128)S(1)} %get-tuple-element.6, f32[512]{0:T(512)S(1)} %bitcast.23, f32[512]{0:T(512)S(1)} %bitcast.22), kind=kLoop, calls=%fused_computation.1 | loop fusion | flops 448000 | bytes 1284096 | tf_op jit(solution)/shard_map/add | solution.py:565

commit v4 on v3

--- a/solution.py
+++ b/solution.py
@@ -328,8 +328,11 @@
     tagged = jnp.where(lanes == FACE_TAG, chosen[:, TAG : TAG + 1], 0.0)
     leaving_low = dot_last(pick, old_halves[0]) + tagged
     leaving_high = dot_last(pick, old_halves[1]) + tagged
-    far_out[0] = leaving_low[:MOVE]
-    far_out[1] = leaving_high[MOVE:]
+    leaving_low = leaving_low[:, :FACE] + leaving_low[:, FACE:]
+    leaving_high = leaving_high[:, :FACE] + leaving_high[:, FACE:]
+    middle = MOVE // 2
+    far_out[0] = jnp.concatenate([leaving_low[:middle], leaving_low[middle:MOVE]], 1)
+    far_out[1] = jnp.concatenate([leaving_high[MOVE : MOVE + middle], leaving_high[MOVE + middle :]], 1)
 
     pl.semaphore_wait(barrier, ranks - 1)
 
@@ -432,9 +435,10 @@
             ghosts = widen(halo_in[turn, face])
             if not turn:
                 gone = leaving_high[:MOVE] if face == 0 else leaving_low[MOVE:]
-                wide = jnp.concatenate([far_in[face], gone], 0)
+                far = far_in[face]
+                wide = jnp.concatenate([far[:, :FACE], far[:, FACE:], gone], 0)
                 hot = one_hot(wide[:, FACE_TAG : FACE_TAG + 1] - 1.0, ghosts[FACE_TAG : FACE_TAG + 1])
-                placed = dot(wide.T.astype(BF), hot)
+                placed = dot(jnp.concatenate(split_two(wide.T), 0), hot)
                 ghosts = ghosts + placed[:FACE] + placed[FACE:]
             received = jnp.concatenate(split_two(ghosts), 0)
             first, second, scaled = coefficients(face, near[face] + dot(received, ghost_hot[face]))
@@ -444,6 +448,9 @@
 
     def down(value):
         return jnp.sum(value, 0, keepdims=True)
+
+    def across(value):
+        return jnp.sum(value, 1, keepdims=True)
 
     def save(index, value):
         basis[index] = value
@@ -458,18 +465,18 @@
     found = []
 
     def early_sums(result):
-        found.append(down(field * field))
-        found.append(down(field * image))
-        found.append(down(image * image))
+        found.append(across(down(field * field)))
+        found.append(across(down(field * image)))
+        found.append(across(down(image * image)))
         found.append(down(image * result))
 
     result, energy, lift = operate(image, 1, early_sums)
-    found[3] = found[3] + energy
+    found[3] = across(found[3] + energy)
 
     lane = iota((1, ROWS), 1)
     message = jnp.zeros((1, ROWS), F32)
     for index, value in enumerate(found):
-        message = jnp.where(lane == index, jnp.sum(value, 1, keepdims=True), message)
+        message = jnp.where(lane == index, value, message)
     sums[0] = message
 
     for_each_other(
@@ -541,8 +548,8 @@
             pltpu.VMEM((2, cells, ghost), BF),
             pltpu.VMEM((2, MOVE, ROWS), F32),
             pltpu.VMEM((2, MOVE, ROWS), F32),
-            pltpu.VMEM((2, MOVE, ROWS), F32),
-            pltpu.VMEM((2, MOVE, ROWS), F32),
+            pltpu.VMEM((2, MOVE // 2, ROWS), F32),
+            pltpu.VMEM((2, MOVE // 2, ROWS), F32),
             pltpu.VMEM((2, 2, HALO, ghost), F32),
             pltpu.VMEM((2, 2, HALO, ghost), F32),
             pltpu.VMEM((ranks, 1, ROWS), F32),

time: 25.9 us -> 25.9 us (level)
  no operation moved by 1% of the time
where the time goes in v4:
time: 25.9 us; the launch traced here: 25.8 us
  Pallas kernels  24.3 us (94%)
  other arithmetic  0.88 us (3%)
  between operations  0.64 us (2%)
    pallas_call x1, Pallas kernels, body(): pl.pallas_call(functools.partial(kernel, shape), out_shape=(jax.ShapeDtyp...  24.3 us
    add x1, other arithmetic, body(): first - linear * second + square * third  0.88 us

profile of v4, /device:TPU:0, one launch (start us, length us, event | category | flops | bytes accessed | tf_op | source)
XLA Modules:
  0.0 25.8 jit_solution(17895127863598484011)
XLA Ops:
  0.6 24.3 %shard_map.104 = (f32[3,128,512]{2,1,0:T(8,128)S(1)}, f32[1,512]{1,0:T(1,128)S(1)}, f32[1,512]{1,0:T(1,128)S(1)}) custom-call(f32[125,512]{1,0:T(8,128)} %rhs_hbm.1, f32[1,512]{1,0:T(1,128)} %bitcast.24, s32[1,512]{1,0:T(1,128)} %bitcast.25, s32[6,512]{1,0:T(8,128)} %neigh_hbm.1, s32[6,512]{1,0:T(8,128)} %orient_hbm.1, s32[2,256]{1,0:T(2,128)} %list_hbm.1, ...), custom_call_target="tpu_custom_call" | custom-call | tf_op jit(solution)/shard_map/pallas_call | solution.py:533
  24.9 0.9 %fusion = (f32[125,512]{1,0:T(8,128)}, f32[125,512]{1,0:T(8,128)}) fusion(f32[3,128,512]{2,1,0:T(8,128)S(1)} %get-tuple-element.6, f32[512]{0:T(512)S(1)} %bitcast.23, f32[512]{0:T(512)S(1)} %bitcast.22), kind=kLoop, calls=%fused_computation.1 | loop fusion | flops 448000 | bytes 1284096 | tf_op jit(solution)/shard_map/add | solution.py:572

commit v5 on v4

--- a/solution.py
+++ b/solution.py
@@ -301,6 +301,25 @@
     packed[0] = chosen[:MOVE]
     packed[1] = chosen[MOVE:]
 
+    pl.semaphore_wait(barrier, ranks - 1)
+
+    def exchange(source, target, send_sem, recv_sem, reach):
+        return [
+            pltpu.make_async_remote_copy(
+                src_ref=source.at[side],
+                dst_ref=target.at[1 - side],
+                send_sem=send_sem.at[side],
+                recv_sem=recv_sem.at[1 - side],
+                device_id=device,
+                device_id_type=MESH,
+            )
+            for side, device in ((0, other(ranks - reach)), (1, other(reach)))
+        ]
+
+    moves = exchange(packed, moved, move_send, move_recv, 1)
+    for copy in moves:
+        copy.start()
+
     for load in loads[4:]:
         load.wait()
 
@@ -334,25 +353,9 @@
     far_out[0] = jnp.concatenate([leaving_low[:middle], leaving_low[middle:MOVE]], 1)
     far_out[1] = jnp.concatenate([leaving_high[MOVE : MOVE + middle], leaving_high[MOVE + middle :]], 1)
 
-    pl.semaphore_wait(barrier, ranks - 1)
-
-    def exchange(source, target, send_sem, recv_sem, reach):
-        return [
-            pltpu.make_async_remote_copy(
-                src_ref=source.at[side],
-                dst_ref=target.at[1 - side],
-                send_sem=send_sem.at[side],
-                recv_sem=recv_sem.at[1 - side],
-                device_id=device,
-                device_id_type=MESH,
-            )
-            for side, device in ((0, other(ranks - reach)), (1, other(reach)))
-        ]
-
-    moves = exchange(packed, moved, move_send, move_recv, 1)
     halos = exchange(halo_out.at[0], halo_in.at[0], halo_send.at[0], halo_recv.at[0], 1)
     fars = exchange(far_out, far_in, far_send, far_recv, 2)
-    for copy in moves + fars + halos:
+    for copy in fars + halos:
         copy.start()
 
     stay = one_hot(iota((cells, cells), 0), offset)

time: 25.9 us -> 25.4 us (0.981)
  Pallas kernels: 24.3 us -> 23.7 us
    pallas_call x1, Pallas kernels: 24.3 us -> 23.7 us  [body(): pl.pallas_call(functools.partial(kernel, shape), out_shape=(jax.ShapeDtyp...]
where the time goes in v5:
time: 25.4 us; the launch traced here: 25.2 us
  Pallas kernels  23.7 us (93%)
  other arithmetic  0.88 us (3%)
  between operations  0.64 us (3%)
    pallas_call x1, Pallas kernels, body(): pl.pallas_call(functools.partial(kernel, shape), out_shape=(jax.ShapeDtyp...  23.7 us
    add x1, other arithmetic, body(): first - linear * second + square * third  0.88 us

profile of v5, /device:TPU:0, one launch (start us, length us, event | category | flops | bytes accessed | tf_op | source)
XLA Modules:
  0.0 25.2 jit_solution(11407972944273594645)
XLA Ops:
  0.6 23.7 %shard_map.104 = (f32[3,128,512]{2,1,0:T(8,128)S(1)}, f32[1,512]{1,0:T(1,128)S(1)}, f32[1,512]{1,0:T(1,128)S(1)}) custom-call(f32[125,512]{1,0:T(8,128)} %rhs_hbm.1, f32[1,512]{1,0:T(1,128)} %bitcast.24, s32[1,512]{1,0:T(1,128)} %bitcast.25, s32[6,512]{1,0:T(8,128)} %neigh_hbm.1, s32[6,512]{1,0:T(8,128)} %orient_hbm.1, s32[2,256]{1,0:T(2,128)} %list_hbm.1, ...), custom_call_target="tpu_custom_call" | custom-call | tf_op jit(solution)/shard_map/pallas_call | solution.py:536
  24.3 0.9 %fusion = (f32[125,512]{1,0:T(8,128)}, f32[125,512]{1,0:T(8,128)}) fusion(f32[3,128,512]{2,1,0:T(8,128)S(1)} %get-tuple-element.6, f32[512]{0:T(512)S(1)} %bitcast.23, f32[512]{0:T(512)S(1)} %bitcast.22), kind=kLoop, calls=%fused_computation.1 | loop fusion | flops 448000 | bytes 1284096 | tf_op jit(solution)/shard_map/add | solution.py:575
